TPU v7x, 32 devices: a whole 2x2x4 slice. The times are simulated.
32 devices in a mesh: dp: 2 (over x), tp: 16 (over y, z, core).
Axes of the slice: x: 2, y: 2, z: 4, core: 2. Of those that a mesh axis runs over, the one named last changes fastest.
Arguments:
- x: bfloat16 [4096, 3072], P('dp'), parts along dimension 0
- dy: bfloat16 [4096, 3072], P('dp'), parts along dimension 0
- gate: bfloat16 [4096, 8192], P('dp', 'tp'), parts along dimension 0
- up: bfloat16 [4096, 8192], P('dp', 'tp'), parts along dimension 0
- w_gate: bfloat16 [3072, 8192], P(None, 'tp')
- w_up: bfloat16 [3072, 8192], P(None, 'tp')
- w_down: bfloat16 [8192, 3072], P('tp')
Outputs:
- output 1: bfloat16 [4096, 3072], P('dp'), parts along dimension 0
- output 2: bfloat16 [6144, 8192], P('dp', 'tp'), parts along dimension 0
- output 3: bfloat16 [6144, 8192], P('dp', 'tp'), parts along dimension 0
- output 4: bfloat16 [16384, 3072], P(('dp', 'tp')), parts along dimension 0
There are 2 independent parts. A program takes and returns all parts, laid end to end along the dimension named above; an argument that names none is the same for every part.
All inputs are finite; a program needn't handle non-finite values.
Results may differ from a plain program's by a relative error of at most 0.012.
Values are sent between devices in bfloat16 or wider.
A program may use at most 2 GiB of HBM per device.

v0:
```python
import jax
import jax.numpy as jnp
from jax import lax
from jax.sharding import PartitionSpec as P


def act(gate, up):
    return jax.nn.silu(gate) * up


def solution(mesh):
    def step(x, dy, gate, up, w_gate, w_up, w_down):
        hidden, back = jax.vjp(act, gate.astype(jnp.float32), up.astype(jnp.float32))
        d_hidden = jnp.dot(dy, w_down.T, preferred_element_type=jnp.float32)
        d_gate, d_up = (g.astype(jnp.bfloat16) for g in back(d_hidden))
        term = jnp.dot(d_gate, w_gate.T, preferred_element_type=jnp.float32) + jnp.dot(d_up, w_up.T, preferred_element_type=jnp.float32)
        dx = lax.psum(term.astype(jnp.bfloat16), "tp")
        dw_gate = jnp.dot(x.T, d_gate, preferred_element_type=jnp.float32)
        dw_up = jnp.dot(x.T, d_up, preferred_element_type=jnp.float32)
        dw_down = jnp.dot(hidden.astype(jnp.bfloat16).T, dy, preferred_element_type=jnp.float32)
        return dx, *(g.astype(jnp.bfloat16) for g in (dw_gate, dw_up, dw_down))

    tokens, columns, rows = P("dp", None), P(None, "tp"), P("tp", None)
    return jax.shard_map(
        step,
        mesh=mesh,
        in_specs=(tokens, tokens, P("dp", "tp"), P("dp", "tp"), columns, columns, rows),
        out_specs=(tokens, P("dp", "tp"), P("dp", "tp"), P(("dp", "tp"), None)),
        check_vma=False,
    )
```

profile of v0, /device:TPU:0, one launch (start us, length us, event | category | flops | bytes accessed | tf_op | source)
XLA Modules:
  0.0 306.5 jit_solution(16817693196909610079)
XLA Ops:
  7.2 0.0 copy-start
  7.2 0.0 all-reduce.2.cloned.1.call-start
  7.2 16.1 %fusion.6 = (bf16[2048,512]{1,0:T(8,128)(2,1)S(1)}, f32[2048,512]{1,0:T(8,128)}) fusion(bf16[2048,512]{1,0:T(8,128)(2,1)} %param.9, bf16[2048,512]{1,0:T(8,128)(2,1)} %param.10, bf16[2048,3072]{1,0:T(8,128)(2,1)} %param.8, bf16[512,3072]{1,0:T(8,128)(2,1)} %param.13), kind=kOutput, calls=%fused_computation.16 | convolution fusion | flops 6456082432 | bytes 26214400 | tf_op jit(solution)/shard_map/dot_general | solution.py:14
  23.3 0.0 copy-start.4
  23.3 0.0 copy-done
  23.3 0.0 copy-start.2
  23.3 0.0 copy-start.3
  23.3 12.0 %fusion.11 = f32[2048,3072]{1,0:T(8,128)} fusion(bf16[2048,512]{1,0:T(8,128)(2,1)S(1)} %get-tuple-element.8, bf16[3072,512]{1,0:T(8,128)(2,1)S(1)} %copy-done), kind=kOutput, calls=%fused_computation.21 | convolution fusion | flops 6442450944 | bytes 30408704 | tf_op jit(solution)/shard_map/dot_general | solution.py:16
  35.3 0.0 copy-done.4
  35.3 0.0 copy-done.2
  35.3 0.0 copy-done.3
  35.3 18.7 %add_convert_fusion = bf16[2048,3072]{1,0:T(8,128)(2,1)} fusion(f32[2048,3072]{1,0:T(8,128)} %fusion.11, bf16[3072,512]{1,0:T(8,128)(2,1)S(1)} %copy-done.2, f32[2048,512]{1,0:T(8,128)} %get-tuple-element.9, bf16[2048,512]{1,0:T(8,128)(2,1)S(1)} %copy-done.3), kind=kOutput, calls=%fused_computation | convolution fusion | flops 6462373888 | bytes 47185920 | tf_op jit(solution)/shard_map/dot_general | solution.py:16
  54.0 0.0 all-reduce.2.cloned.1.call-update
  54.0 10.6 %fusion.7 = bf16[3072,512]{0,1:T(8,128)(2,1)S(1)} fusion(bf16[2048,512]{1,0:T(8,128)(2,1)} %copy-done.4, bf16[2048,3072]{1,0:T(8,128)(2,1)} %param.7), kind=kOutput, calls=%fused_computation.18 | convolution fusion | flops 6444023808 | bytes 17825792 | tf_op jit(solution)/shard_map/dot_general | solution.py:18
  64.6 2.8 copy.11
  67.4 13.0 %fusion.8 = bf16[3072,512]{0,1:T(8,128)(2,1)S(1)} fusion(bf16[2048,3072]{1,0:T(8,128)(2,1)} %param.7, f32[2048,512]{1,0:T(8,128)} %get-tuple-element.9, bf16[2048,512]{1,0:T(8,128)(2,1)} %param.9), kind=kOutput, calls=%fused_computation.19 | convolution fusion | flops 6451363840 | bytes 22020096 | tf_op jit(solution)/shard_map/dot_general | solution.py:19
  80.4 2.8 copy.12
  83.2 12.6 %convolution_convert_fusion = bf16[512,3072]{1,0:T(8,128)(2,1)} fusion(bf16[2048,3072]{1,0:T(8,128)(2,1)} %param.8, bf16[2048,512]{1,0:T(8,128)(2,1)} %param.10, bf16[2048,512]{1,0:T(8,128)(2,1)} %param.9), kind=kOutput, calls=%fused_computation.7 | convolution fusion | flops 6452412416 | bytes 19922944 | tf_op jit(solution)/shard_map/dot_general | solution.py:20
  95.8 193.0 %all-reduce.2.cloned.1.call-done = bf16[2048,3072]{1,0:T(8,128)(2,1)} async-done(((bf16[2048,3072]{1,0:T(8,128)(2,1)}), bf16[2048,3072]{1,0:T(8,128)(2,1)}) %all-reduce.2.cloned.1.call-update) | async-done | bytes 12582928 | tf_op jit(solution)/shard_map/psum | solution.py:17
  288.8 0.0 copy-start.1
  288.9 10.8 %copy.14 = bf16[2048,3072]{1,0:T(8,128)(2,1)} copy(bf16[2048,3072]{1,0:T(8,128)(2,1)} %all-reduce.2.cloned.1.call-done) | data formatting | bytes 25165824
  299.6 0.0 copy-done.1
Async XLA Ops:
  7.2 16.1 %copy-start = (bf16[3072,512]{1,0:T(8,128)(2,1)S(1)}, bf16[3072,512]{1,0:T(8,128)(2,1)}, u32[]{:S(2)}) copy-start(bf16[3072,512]{1,0:T(8,128)(2,1)} %param.11) | copy-start | bytes 9437188
  7.2 281.7 %all-reduce.2.cloned.1.call-start = ((), (), s32[]{:S(2)}) async-start(), calls=%async_computation | async-start | bytes 25165824 | tf_op jit(solution)/shard_map/psum | solution.py:17
  23.3 12.0 %copy-start.4 = (bf16[2048,512]{1,0:T(8,128)(2,1)}, bf16[2048,512]{1,0:T(8,128)(2,1)S(1)}, u32[]{:S(2)}) copy-start(bf16[2048,512]{1,0:T(8,128)(2,1)S(1)} %get-tuple-element.8) | copy-start | bytes 6291460
  23.3 12.0 %copy-start.2 = (bf16[3072,512]{1,0:T(8,128)(2,1)S(1)}, bf16[3072,512]{1,0:T(8,128)(2,1)}, u32[]{:S(2)}) copy-start(bf16[3072,512]{1,0:T(8,128)(2,1)} %param.12) | copy-start | bytes 9437188
  23.3 12.0 %copy-start.3 = (bf16[2048,512]{1,0:T(8,128)(2,1)S(1)}, bf16[2048,512]{1,0:T(8,128)(2,1)}, u32[]{:S(2)}) copy-start(bf16[2048,512]{1,0:T(8,128)(2,1)} %param.9) | copy-start | bytes 6291460
  288.8 10.8 %copy-start.1 = (bf16[3072,512]{1,0:T(8,128)(2,1)S(1)}, bf16[3072,512]{1,0:T(8,128)(2,1)}, u32[]{:S(2)}) copy-start(bf16[3072,512]{1,0:T(8,128)(2,1)} %param.11) | copy-start | bytes 9437188
Sparse Core Ops, SparseCore 0:
  54.1 234.6 all-reduce.1
where the time goes:
time: 307 us; the launch traced here: 306 us
  waiting for transfers between devices  193 us (63%)
  matrix products  82.9 us (27%)
  local copies, waits for them, and re-layouts  16.4 us (5%)
  between operations  14.1 us (5%)
    psum x1, waiting for transfers between devices, step(): dx = lax.psum(term.astype(jnp.bfloat16), 'tp')  193 us
    dot_general x1, matrix products, step(): jnp.dot(d_up, w_up.T, preferred_element_type=jnp.float32)  18.7 us
    unnamed x13, local copies, waits for them, and re-layouts  16.4 us
    dot_general x1, matrix products, step(): d_hidden = jnp.dot(dy, w_down.T, preferred_element_type=jnp.float32)  16.1 us
    dot_general x1, matrix products, step(): dw_up = jnp.dot(x.T, d_up, preferred_element_type=jnp.float32)  13 us
    dot_general x1, matrix products, step(): jnp.dot(hidden.astype(jnp.bfloat16).T, dy, preferred_element_type=jnp.flo...  12.6 us
    dot_general x1, matrix products, step(): jnp.dot(d_gate, w_gate.T, preferred_element_type=jnp.float32)  12 us
    dot_general x1, matrix products, step(): dw_gate = jnp.dot(x.T, d_gate, preferred_element_type=jnp.float32)  10.6 us
  transfers between devices with their start and end apart: 1, of which 1 were waited for; matrix products, arithmetic and copies ran while one was open for 14% of the time, Pallas kernels for 0%

commit v1 on v0

v1 whole, which is shorter than its diff:
```python
import jax
import jax.numpy as jnp
from jax import lax
from jax.experimental import pallas as pl
from jax.experimental.pallas import tpu as pltpu
from jax.sharding import PartitionSpec as P

MESH = pl.DeviceIdType.MESH
F32, BF16 = jnp.float32, jnp.bfloat16

TOKENS, D, HID = 2048, 3072, 512
HALF = TOKENS // 2
CHIPS = 8
ROWS = HALF // CHIPS
Q = 4
COLS = D // Q
TILE = 256
TILES = D // TILE


def dot(a, b, contract):
    return lax.dot_general(a, b, (contract, ((), ())), preferred_element_type=F32)


def ring_kernel(
    x, dy, gate, up, w_gate, w_up, w_down,
    dx, dw_gate, dw_up, dw_down,
    wg, wu, wd, dyt, gt, ut, xt, own, stage, dgu, hid,
    w_sem, t_sem, x_sem, free,
    sib_s, sib_r, rs_s, rs_r, ag_s, ag_r, fin_s, fin_r,
):
    me = lax.axis_index("tp")
    core = lax.rem(me, 2)
    chip = me // 2
    y, z = chip // 4, lax.rem(chip, 4)
    pos = z + y * (7 - 2 * z)
    turn = 1 - 2 * core

    def device(position, c):
        p = lax.rem(position + CHIPS, CHIPS)
        back = p // 4
        zz = p + back * (7 - 2 * p)
        return (back * 4 + zz) * 2 + c

    down, upstream = device(pos + turn, core), device(pos - turn, core)
    sibling = me + turn

    for name, src, dst in ((0, w_down, wd), (1, w_gate, wg), (2, w_up, wu)):
        pltpu.make_async_copy(src, dst, w_sem.at[name]).start()

    def chunk(t, c_turn):
        return lax.rem(pos - c_turn * t + 2 * CHIPS, CHIPS)

    def mine(t):
        return pl.multiple_of(core * HALF + chunk(t, turn) * ROWS, ROWS)

    def theirs(t):
        return pl.multiple_of((1 - core) * HALF + chunk(t, -turn) * ROWS, ROWS)

    def landing(t, c):
        return pl.multiple_of((1 - c) * HALF + t * ROWS, ROWS)

    def tiles(t):
        slot = lax.rem(t, 2)
        out = []
        for k, (src, dst) in enumerate(((dy, dyt), (gate, gt), (up, ut))):
            for h, r in enumerate((mine(t), theirs(t))):
                out.append(pltpu.make_async_copy(
                    src.at[pl.ds(r, ROWS)], dst.at[slot, pl.ds(h * ROWS, ROWS)],
                    t_sem.at[slot, 2 * k + h]))
        return out

    def load(t):
        for c in tiles(t):
            c.start()

    load(0)

    barrier = pltpu.get_barrier_semaphore()
    for d in (down, upstream, sibling):
        pl.semaphore_signal(barrier, inc=1, device_id={"tp": d}, device_id_type=MESH)
    pl.semaphore_wait(barrier, 3)

    def remote(src, dst, s, r, to):
        return pltpu.make_async_remote_copy(
            src_ref=src, dst_ref=dst, send_sem=s, recv_sem=r,
            device_id={"tp": to}, device_id_type=MESH)

    def signal(k, to):
        pl.semaphore_signal(free.at[k], inc=1, device_id={"tp": to}, device_id_type=MESH)

    def cols(q):
        return pl.ds(pl.multiple_of(q * COLS, COLS), COLS)

    def sib_copy(t, q):
        return remote(stage.at[lax.rem(t, 2), :, cols(q)],
                      dx.at[pl.ds(landing(t, 1 - core), ROWS), cols(q)],
                      sib_s.at[t, q], sib_r.at[t, q], sibling)

    def sib_wait(t, q):
        return remote(stage.at[lax.rem(t, 2), :, cols(q)],
                      dx.at[pl.ds(landing(t, core), ROWS), cols(q)],
                      sib_s.at[t, q], sib_r.at[t, q], sibling)

    def rs_copy(t, q):
        at = dx.at[pl.ds(mine(t), ROWS), cols(q)]
        return remote(at, at, rs_s.at[t, q], rs_r.at[t, q], down)

    def rs_wait(t, q):
        at = dx.at[pl.ds(mine(t + 1), ROWS), cols(q)]
        return remote(at, at, rs_s.at[t, q], rs_r.at[t, q], down)

    def ag_copy(t, q):
        at = dx.at[pl.ds(mine(t + 7), ROWS), cols(q)]
        return remote(at, at, ag_s.at[t, q], ag_r.at[t, q], down)

    def ag_wait(t, q):
        at = dx.at[pl.ds(mine(t + 8), ROWS), cols(q)]
        return remote(at, at, ag_s.at[t, q], ag_r.at[t, q], down)

    def fin_copy(t, q):
        at = dx.at[pl.ds(mine(t + 7), ROWS), cols(q)]
        return remote(at, at, fin_s.at[t, q], fin_r.at[t, q], sibling)

    def fin_wait(t, q):
        at = dx.at[pl.ds(theirs(t + 7), ROWS), cols(q)]
        return remote(at, at, fin_s.at[t, q], fin_r.at[t, q], sibling)

    def hidden_part(t):
        slot = lax.rem(t, 2)
        for c in tiles(t):
            c.wait()

        @pl.when(t == 0)
        def _():
            pltpu.make_async_copy(w_down, wd, w_sem.at[0]).wait()

        dh = dot(dyt[slot], wd[...], ((1,), (1,)))
        g, u = gt[slot].astype(F32), ut[slot].astype(F32)
        sig = jax.nn.sigmoid(g)
        silu = g * sig
        d_up = (dh * silu).astype(BF16)
        d_gate = (dh * u * (sig * (1 + g * (1 - sig)))).astype(BF16)
        h = (silu * u).astype(BF16)
        for k, r in enumerate((mine(t), theirs(t))):
            at, part = pl.ds(r, ROWS), slice(k * ROWS, (k + 1) * ROWS)
            dgu[at, :HID] = d_gate[part]
            dgu[at, HID:] = d_up[part]
            hid[at] = h[part]

        @pl.when(t == 0)
        def _():
            pltpu.make_async_copy(w_gate, wg, w_sem.at[1]).wait()
            pltpu.make_async_copy(w_up, wu, w_sem.at[2]).wait()

    def term_part(t, q):
        slot = lax.rem(t, 2)
        a = jnp.concatenate([dgu[pl.ds(mine(t), ROWS)], dgu[pl.ds(theirs(t), ROWS)]], axis=0)
        v = (dot(a[:, :HID], wg[q * COLS:(q + 1) * COLS], ((1,), (1,)))
             + dot(a[:, HID:], wu[q * COLS:(q + 1) * COLS], ((1,), (1,))))

        @pl.when(t >= 2)
        def _():
            sib_copy(t - 2, q).wait_send()

        stage[slot, :, q * COLS:(q + 1) * COLS] = v[ROWS:].astype(BF16)
        sib_copy(t, q).start()
        own[slot, :, q * COLS:(q + 1) * COLS] = v[:ROWS]

    def sum_part(t, q):
        slot = lax.rem(t, 2)
        at = pl.ds(mine(t), ROWS)
        sib_wait(t, q).wait_recv()
        c = slice(q * COLS, (q + 1) * COLS)

        def local():
            return own[slot, :, c] + dx[pl.ds(landing(t, core), ROWS), c].astype(F32)

        @pl.when(t == 0)
        def _():
            dx[at, c] = local().astype(BF16)

        @pl.when(t > 0)
        def _():
            rs_wait(t - 1, q).wait_recv()
            rs_copy(t - 1, q).wait_send()
            dx[at, c] = (local() + dx[at, c].astype(F32)).astype(BF16)

        @pl.when(t < CHIPS - 1)
        def _():
            rs_copy(t, q).start()

        @pl.when(t == CHIPS - 1)
        def _():
            ag_copy(0, q).start()

    def xtile(i):
        slot = lax.rem(i, 2)
        return lambda src: pltpu.make_async_copy(
            src.at[:, pl.ds(pl.multiple_of(lax.rem(i, TILES) * TILE, TILE), TILE)],
            xt.at[slot], x_sem.at[slot])

    def load_x(i):
        @pl.when(i < TILES)
        def _():
            xtile(i)(x).start()

        @pl.when((i >= TILES) & (i < 2 * TILES))
        def _():
            xtile(i)(dy).start()

    load(1)
    hidden_part(0)
    for q in range(Q):
        term_part(0, q)

    def rs_stage(t, carry):
        @pl.when(t + 1 < CHIPS)
        def _():
            load(t + 1)

        hidden_part(t)
        for q in range(Q):
            term_part(t, q)
            sum_part(t - 1, q)
        return carry

    lax.fori_loop(1, CHIPS, rs_stage, 0)
    load_x(0)
    signal(1, upstream)
    pl.semaphore_wait(free.at[1], 1)
    for q in range(Q):
        sum_part(CHIPS - 1, q)
    signal(0, sibling)
    signal(2, upstream)
    pl.semaphore_wait(free.at[0], 1)
    for q in range(Q):
        fin_copy(0, q).start()

    def ag_step(i, carry):
        t, q = i // Q, lax.rem(i, Q)
        slot = lax.rem(i, 2)
        load_x(i + 1)

        @pl.when(i < 2 * TILES)
        def _():
            xtile(i)(x).wait()

        at = pl.ds(pl.multiple_of(lax.rem(i, TILES) * TILE, TILE), TILE)

        @pl.when(i < TILES)
        def _():
            v = dot(xt[slot], dgu[...], ((0,), (0,))).astype(BF16)
            dw_gate[at] = v[:, :HID]
            dw_up[at] = v[:, HID:]

        @pl.when((i >= TILES) & (i < 2 * TILES))
        def _():
            dw_down[:, at] = dot(hid[...], xt[slot], ((0,), (0,))).astype(BF16)

        ag_wait(t, q).wait_recv()

        @pl.when(i == (CHIPS - 3) * Q)
        def _():
            pl.semaphore_wait(free.at[2], 1)

        @pl.when(t < CHIPS - 2)
        def _():
            ag_copy(t + 1, q).start()

        fin_copy(t + 1, q).start()
        return carry

    lax.fori_loop(0, (CHIPS - 1) * Q, ag_step, 0)

    def drain(i, carry):
        t, q = i // Q, lax.rem(i, Q)

        @pl.when(t < CHIPS - 1)
        def _():
            ag_copy(t, q).wait_send()

        @pl.when(t >= CHIPS - 2)
        def _():
            sib_copy(t, q).wait_send()

        fin_copy(t, q).wait_send()
        fin_wait(t, q).wait_recv()
        return carry

    lax.fori_loop(0, CHIPS * Q, drain, 0)


def flush_kernel(*refs):
    sem = refs[-1]
    n = (len(refs) - 1) // 2
    copies = [pltpu.make_async_copy(refs[k], refs[n + k], sem.at[k]) for k in range(n)]
    for c in copies:
        c.start()
    for c in copies:
        c.wait()


def solution(mesh):
    dma = pltpu.SemaphoreType.DMA
    shapes = ((TOKENS, D), (D, HID), (D, HID), (HID, D))

    def step(x, dy, gate, up, w_gate, w_up, w_down):
        hbm = pl.BlockSpec(memory_space=pltpu.HBM)
        vmem = pl.BlockSpec(memory_space=pltpu.VMEM)
        held = pl.pallas_call(
            ring_kernel,
            out_shape=tuple(pltpu.VMEM(s, BF16) for s in shapes),
            in_specs=[hbm] * 7,
            out_specs=(vmem,) * 4,
            scratch_shapes=[
                pltpu.VMEM((D, HID), BF16), pltpu.VMEM((D, HID), BF16), pltpu.VMEM((HID, D), BF16),
                pltpu.VMEM((2, 2 * ROWS, D), BF16),
                pltpu.VMEM((2, 2 * ROWS, HID), BF16), pltpu.VMEM((2, 2 * ROWS, HID), BF16),
                pltpu.VMEM((2, TOKENS, TILE), BF16),
                pltpu.VMEM((2, ROWS, D), F32), pltpu.VMEM((2, ROWS, D), BF16),
                pltpu.VMEM((TOKENS, 2 * HID), BF16), pltpu.VMEM((TOKENS, HID), BF16),
                dma((3,)), dma((2, 6)), dma((2,)), pltpu.SemaphoreType.REGULAR((3,)),
                dma((CHIPS, Q)), dma((CHIPS, Q)),
                dma((CHIPS - 1, Q)), dma((CHIPS - 1, Q)),
                dma((CHIPS - 1, Q)), dma((CHIPS - 1, Q)),
                dma((CHIPS, Q)), dma((CHIPS, Q)),
            ],
            compiler_params=pltpu.CompilerParams(
                collective_id=0, has_side_effects=True, vmem_limit_bytes=40 * 2**20),
        )(x, dy, gate, up, w_gate, w_up, w_down)
        return pl.pallas_call(
            flush_kernel,
            out_shape=tuple(jax.ShapeDtypeStruct(s, BF16) for s in shapes),
            in_specs=[vmem] * 4,
            out_specs=(hbm,) * 4,
            scratch_shapes=[dma((4,))],
            compiler_params=pltpu.CompilerParams(vmem_limit_bytes=2 * 2**20),
        )(*held)

    tokens, columns, rows = P("dp", None), P(None, "tp"), P("tp", None)
    return jax.shard_map(
        step,
        mesh=mesh,
        in_specs=(tokens, tokens, P("dp", "tp"), P("dp", "tp"), columns, columns, rows),
        out_specs=(tokens, P("dp", "tp"), P("dp", "tp"), P(("dp", "tp"), None)),
        check_vma=False,
    )
```

time: 307 us -> 145 us (0.47)
  waiting for transfers between devices: 193 us -> 0 us
  Pallas kernels: 0 us -> 144 us
  matrix products: 82.9 us -> 0 us
  local copies, waits for them, and re-layouts: 16.4 us -> 0 us
  between operations: 14.1 us -> 0.64 us
    psum x1 -> x0, waiting for transfers between devices: 193 us -> none  [step(): dx = lax.psum(term.astype(jnp.bfloat16), 'tp')]
    pallas_call x0 -> x2, Pallas kernels: none -> 144 us  [the longest x1 137 us: step(): pl.pallas_call(ring_kernel, out_shape=tuple((pltpu.VMEM(s, BF16) for s in...]
    dot_general x6 -> x0, matrix products: 82.9 us -> none  [the longest x1 18.7 us: step(): jnp.dot(d_up, w_up.T, preferred_element_type=jnp.float32)]
    unnamed x13 -> x0, local copies, waits for them, and re-layouts: 16.4 us -> none
  transfers between devices with their start and end apart: 1 -> 0, of which waited for: 1 -> 0; matrix products, arithmetic and copies ran while one was open for 14% -> 0% of each run, Pallas kernels for 0% -> 0%
where the time goes in v1:
time: 145 us
  Pallas kernels  144 us (99%)
    pallas_call x1, Pallas kernels, step(): pl.pallas_call(ring_kernel, out_shape=tuple((pltpu.VMEM(s, BF16) for s in...  137 us
    pallas_call x1, Pallas kernels, step(): pl.pallas_call(flush_kernel, out_shape=tuple((jax.ShapeDtypeStruct(s, BF1...  7.73 us

profile of v1, /device:TPU:0, one launch (start us, length us, event | category | flops | bytes accessed | tf_op | source)
XLA Modules:
  0.0 144.9 jit_solution(1827181206956579063)
XLA Ops:
  0.6 136.5 %shard_map.102 = (bf16[2048,3072]{1,0:T(8,128)(2,1)S(1)}, bf16[3072,512]{1,0:T(8,128)(2,1)S(1)}, bf16[3072,512]{1,0:T(8,128)(2,1)S(1)}, bf16[512,3072]{1,0:T(8,128)(2,1)S(1)}) custom-call(bf16[2048,3072]{1,0:T(8,128)(2,1)} %x.1, bf16[2048,3072]{1,0:T(8,128)(2,1)} %dy.1, bf16[2048,512]{1,0:T(8,128)(2,1)} %gate.1, bf16[2048,512]{1,0:T(8,128)(2,1)} %up.1, ...), custom_call_target="tpu_custom_call" | custom-call | tf_op jit(solution)/shard_map/pallas_call | solution.py:311
  137.2 7.7 %shard_map.103 = (bf16[2048,3072]{1,0:T(8,128)(2,1)}, bf16[3072,512]{1,0:T(8,128)(2,1)}, bf16[3072,512]{1,0:T(8,128)(2,1)}, bf16[512,3072]{1,0:T(8,128)(2,1)}) custom-call(bf16[2048,3072]{1,0:T(8,128)(2,1)S(1)} %get-tuple-element.8.refs_0_, bf16[3072,512]{1,0:T(8,128)(2,1)S(1)} %get-tuple-element.9.refs_1_, bf16[3072,512]{1,0:T(8,128)(2,1)S(1)} %get-tuple-element.10.refs_2_, ...), custom_call_target="tpu_custom_call" | custom-call | tf_op jit(solution)/shard_map/pallas_call | solution.py:332

commit v2 on v1

--- a/solution.py
+++ b/solution.py
@@ -16,6 +16,7 @@
 COLS = D // Q
 TILE = 256
 TILES = D // TILE
+PARTS = 4
 
 
 def dot(a, b, contract):
@@ -45,8 +46,9 @@
     down, upstream = device(pos + turn, core), device(pos - turn, core)
     sibling = me + turn
 
-    for name, src, dst in ((0, w_down, wd), (1, w_gate, wg), (2, w_up, wu)):
-        pltpu.make_async_copy(src, dst, w_sem.at[name]).start()
+    weights = [pltpu.make_async_copy(src, dst, w_sem.at[k])
+               for k, (src, dst) in enumerate(((w_down, wd), (w_gate, wg), (w_up, wu)))]
+    weights[0].start()
 
     def chunk(t, c_turn):
         return lax.rem(pos - c_turn * t + 2 * CHIPS, CHIPS)
@@ -75,6 +77,8 @@
             c.start()
 
     load(0)
+    weights[1].start()
+    weights[2].start()
 
     barrier = pltpu.get_barrier_semaphore()
     for d in (down, upstream, sibling):
@@ -130,11 +134,6 @@
         slot = lax.rem(t, 2)
         for c in tiles(t):
             c.wait()
-
-        @pl.when(t == 0)
-        def _():
-            pltpu.make_async_copy(w_down, wd, w_sem.at[0]).wait()
-
         dh = dot(dyt[slot], wd[...], ((1,), (1,)))
         g, u = gt[slot].astype(F32), ut[slot].astype(F32)
         sig = jax.nn.sigmoid(g)
@@ -148,11 +147,6 @@
             dgu[at, HID:] = d_up[part]
             hid[at] = h[part]
 
-        @pl.when(t == 0)
-        def _():
-            pltpu.make_async_copy(w_gate, wg, w_sem.at[1]).wait()
-            pltpu.make_async_copy(w_up, wu, w_sem.at[2]).wait()
-
     def term_part(t, q):
         slot = lax.rem(t, 2)
         a = jnp.concatenate([dgu[pl.ds(mine(t), ROWS)], dgu[pl.ds(theirs(t), ROWS)]], axis=0)
@@ -209,28 +203,36 @@
         def _():
             xtile(i)(dy).start()
 
-    load(1)
-    hidden_part(0)
-    for q in range(Q):
-        term_part(0, q)
-
-    def rs_stage(t, carry):
-        @pl.when(t + 1 < CHIPS)
-        def _():
-            load(t + 1)
-
-        hidden_part(t)
+    def rs_stage(t):
         for q in range(Q):
             term_part(t, q)
-            sum_part(t - 1, q)
+            if q:
+                sum_part(t, q - 1)
+        sum_part(t, Q - 1)
+
+    def rs_body(t, carry):
+        @pl.when(t + 1 < CHIPS)
+        def _():
+            load(t + 1)
+
+        hidden_part(t)
+
+        @pl.when(t == CHIPS - 1)
+        def _():
+            load_x(0)
+            signal(1, upstream)
+            pl.semaphore_wait(free.at[1], 1)
+
+        rs_stage(t)
         return carry
 
-    lax.fori_loop(1, CHIPS, rs_stage, 0)
-    load_x(0)
-    signal(1, upstream)
-    pl.semaphore_wait(free.at[1], 1)
-    for q in range(Q):
-        sum_part(CHIPS - 1, q)
+    weights[0].wait()
+    hidden_part(0)
+    load(1)
+    weights[1].wait()
+    weights[2].wait()
+    rs_stage(0)
+    lax.fori_loop(1, CHIPS, rs_body, 0)
     signal(0, sibling)
     signal(2, upstream)
     pl.semaphore_wait(free.at[0], 1)
@@ -294,7 +296,12 @@
 def flush_kernel(*refs):
     sem = refs[-1]
     n = (len(refs) - 1) // 2
-    copies = [pltpu.make_async_copy(refs[k], refs[n + k], sem.at[k]) for k in range(n)]
+    copies = []
+    for k in range(n):
+        rows = refs[k].shape[0] // PARTS
+        for p in range(PARTS):
+            at = pl.ds(p * rows, rows)
+            copies.append(pltpu.make_async_copy(refs[k].at[at], refs[n + k].at[at], sem.at[k, p]))
     for c in copies:
         c.start()
     for c in copies:
@@ -334,7 +341,7 @@
             out_shape=tuple(jax.ShapeDtypeStruct(s, BF16) for s in shapes),
             in_specs=[vmem] * 4,
             out_specs=(hbm,) * 4,
-            scratch_shapes=[dma((4,))],
+            scratch_shapes=[dma((4, PARTS))],
             compiler_params=pltpu.CompilerParams(vmem_limit_bytes=2 * 2**20),
         )(*held)
 

time: 145 us -> 140 us (0.966)
  Pallas kernels: 144 us -> 140 us
    pallas_call x1, Pallas kernels: 137 us -> 132 us  [step(): pl.pallas_call(ring_kernel, out_shape=tuple((pltpu.VMEM(s, BF16) for s in...]
where the time goes in v2:
time: 140 us
  Pallas kernels  140 us (100%)
    pallas_call x1, Pallas kernels, step(): pl.pallas_call(ring_kernel, out_shape=tuple((pltpu.VMEM(s, BF16) for s in...  132 us
    pallas_call x1, Pallas kernels, step(): pl.pallas_call(flush_kernel, out_shape=tuple((jax.ShapeDtypeStruct(s, BF1...  7.59 us

profile of v2, /device:TPU:0, one launch (start us, length us, event | category | flops | bytes accessed | tf_op | source)
XLA Modules:
  0.0 140.3 jit_solution(2767321295535106811)
XLA Ops:
  0.6 132.0 %shard_map.102 = (bf16[2048,3072]{1,0:T(8,128)(2,1)S(1)}, bf16[3072,512]{1,0:T(8,128)(2,1)S(1)}, bf16[3072,512]{1,0:T(8,128)(2,1)S(1)}, bf16[512,3072]{1,0:T(8,128)(2,1)S(1)}) custom-call(bf16[2048,3072]{1,0:T(8,128)(2,1)} %x.1, bf16[2048,3072]{1,0:T(8,128)(2,1)} %dy.1, bf16[2048,512]{1,0:T(8,128)(2,1)} %gate.1, bf16[2048,512]{1,0:T(8,128)(2,1)} %up.1, ...), custom_call_target="tpu_custom_call" | custom-call | tf_op jit(solution)/shard_map/pallas_call | solution.py:318
  132.7 7.6 %shard_map.103 = (bf16[2048,3072]{1,0:T(8,128)(2,1)}, bf16[3072,512]{1,0:T(8,128)(2,1)}, bf16[3072,512]{1,0:T(8,128)(2,1)}, bf16[512,3072]{1,0:T(8,128)(2,1)}) custom-call(bf16[2048,3072]{1,0:T(8,128)(2,1)S(1)} %get-tuple-element.8.refs_0_, bf16[3072,512]{1,0:T(8,128)(2,1)S(1)} %get-tuple-element.9.refs_1_, bf16[3072,512]{1,0:T(8,128)(2,1)S(1)} %get-tuple-element.10.refs_2_, ...), custom_call_target="tpu_custom_call" | custom-call | tf_op jit(solution)/shard_map/pallas_call | solution.py:339

commit v3 on v2

v3 whole, which is shorter than its diff:
```python
import jax
import jax.numpy as jnp
from jax import lax
from jax.experimental import pallas as pl
from jax.experimental.pallas import tpu as pltpu
from jax.sharding import PartitionSpec as P

MESH = pl.DeviceIdType.MESH
F32, BF16 = jnp.float32, jnp.bfloat16

TOKENS, D, HID = 2048, 3072, 512
HALF = TOKENS // 2
STAGES = 8
ROWS = HALF // STAGES
BLOCK = ROWS // 4
Q = 4
COLS = D // Q
UNITS = 2 * STAGES
WIDE = D // 2
WA = 896
WB = WIDE - WA
TILE = 256
TILES = D // TILE
PARTS = 4

END = dict(loc=2.0, lA=4.64, lB=2.47, Amo=11.33, Bse=10.53, Ams=32.77, Bse2=36.9, bAmo=43.27, fin=50)
MID = dict(loc=2.0, lA=7.27, Bo=2.1, Amo=11.74, Bs=4.3, Ams=13.66, Bsm2=6.12, bAms=33.59, bAmo=36.27,
           bBse=39.43, bBom=9.75, bBoe=45.08, fin=49.7)
LOOPS = UNITS + max(int(o) // 2 for o in (*END.values(), *MID.values()))


def dot(a, b, contract):
    return lax.dot_general(a, b, (contract, ((), ())), preferred_element_type=F32)


def tree_kernel(
    x, dy, gate, up, w_gate, w_up, w_down,
    dx, dw_gate, dw_up, dw_down,
    dyt, gt, ut, xt, loc, stage, dgu, hid, lz, lr, lx,
    w_sem, t_sem, x_sem, free,
    sib_s, sib_r, fin_s, fin_r, sA, sB, rrA, rzA, bA, rzB, rxB, rrB, bB,
):
    me = lax.axis_index("tp")
    core = lax.rem(me, 2)
    chip = me // 2
    y, z = chip // 4, lax.rem(chip, 4)
    side = z // 2
    o, n = 1 - side, 1 - y
    is_end = z * (3 - z) == 0
    is_mid = z * (3 - z) > 0
    inward = 1 - 2 * side
    sibling = me + 1 - 2 * core

    def device(yy, zz):
        return (yy * 4 + zz) * 2 + core

    rung, inner, outer = device(n, z), device(y, z + inward), device(y, z - inward)

    wg, wu, wd = dw_gate, dw_up, dw_down
    weights = [pltpu.make_async_copy(src, dst, w_sem.at[k])
               for k, (src, dst) in enumerate(((w_down, wd), (w_gate, wg), (w_up, wu)))]
    weights[0].start()

    def mine(t):
        return pl.multiple_of(core * HALF + t * ROWS, ROWS)

    def theirs(t):
        return pl.multiple_of((1 - core) * HALF + t * ROWS, ROWS)

    def tiles(t):
        slot = lax.rem(t, 2)
        out = []
        for k, (src, dst) in enumerate(((dy, dyt), (gate, gt), (up, ut))):
            for h, r in enumerate((mine(t), theirs(t))):
                out.append(pltpu.make_async_copy(
                    src.at[pl.ds(r, ROWS)], dst.at[slot, pl.ds(h * ROWS, ROWS)],
                    t_sem.at[slot, 2 * k + h]))
        return out

    def load(t):
        for c in tiles(t):
            c.start()

    load(0)
    weights[1].start()
    weights[2].start()

    barrier = pltpu.get_barrier_semaphore()

    def greet(d):
        pl.semaphore_signal(barrier, inc=1, device_id={"tp": d}, device_id_type=MESH)

    for d in (rung, inner, sibling):
        greet(d)

    @pl.when(is_mid)
    def _():
        greet(outer)
        pl.semaphore_wait(barrier, 4)

    @pl.when(is_end)
    def _():
        pl.semaphore_wait(barrier, 3)

    def remote(src, dst, s, r, to):
        return pltpu.make_async_remote_copy(
            src_ref=src, dst_ref=dst, send_sem=s, recv_sem=r,
            device_id={"tp": to}, device_id_type=MESH)

    def cols(q):
        return pl.ds(pl.multiple_of(q * COLS, COLS), COLS)

    def sib_copy(t, q):
        return remote(stage.at[lax.rem(t, 2), :, cols(q)], dx.at[pl.ds(mine(t), ROWS), cols(q)],
                      sib_s.at[t, q], sib_r.at[t, q], sibling)

    def sib_wait(t, q):
        at = dx.at[pl.ds(theirs(t), ROWS), cols(q)]
        return remote(at, at, sib_s.at[t, q], sib_r.at[t, q], sibling)

    def hidden_part(t):
        slot = lax.rem(t, 2)
        for c in tiles(t):
            c.wait()
        dh = dot(dyt[slot], wd[...], ((1,), (1,)))
        g, u = gt[slot].astype(F32), ut[slot].astype(F32)
        sig = jax.nn.sigmoid(g)
        silu = g * sig
        d_up = (dh * silu).astype(BF16)
        d_gate = (dh * u * (sig * (1 + g * (1 - sig)))).astype(BF16)
        h = (silu * u).astype(BF16)
        for k, r in enumerate((mine(t), theirs(t))):
            at, part = pl.ds(r, ROWS), slice(k * ROWS, (k + 1) * ROWS)
            dgu[at, :HID] = d_gate[part]
            dgu[at, HID:] = d_up[part]
            hid[at] = h[part]

    def term_part(t, q):
        slot = lax.rem(t, 2)
        a = jnp.concatenate([dgu[pl.ds(mine(t), ROWS)], dgu[pl.ds(theirs(t), ROWS)]], axis=0)
        v = (dot(a[:, :HID], wg[cols(q)], ((1,), (1,)))
             + dot(a[:, HID:], wu[cols(q)], ((1,), (1,))))

        @pl.when(t >= 2)
        def _():
            sib_copy(t - 2, q).wait_send()

        stage[slot, :, cols(q)] = v[ROWS:].astype(BF16)
        sib_copy(t, q).start()
        loc[pl.ds(pl.multiple_of(t * ROWS, ROWS), ROWS), cols(q)] = v[:ROWS]

    def xtile(i):
        slot = lax.rem(i, 2)
        return lambda src: pltpu.make_async_copy(
            src.at[:, pl.ds(pl.multiple_of(lax.rem(i, TILES) * TILE, TILE), TILE)],
            xt.at[slot], x_sem.at[slot])

    def load_x(i):
        @pl.when(i < TILES)
        def _():
            xtile(i)(x).start()

        @pl.when((i >= TILES) & (i < 2 * TILES))
        def _():
            xtile(i)(dy).start()

    def grad_part(i):
        slot = lax.rem(i, 2)
        load_x(i + 1)
        xtile(i)(x).wait()
        at = pl.ds(pl.multiple_of(lax.rem(i, TILES) * TILE, TILE), TILE)

        @pl.when(i < TILES)
        def _():
            v = dot(xt[slot], dgu[...], ((0,), (0,))).astype(BF16)
            dw_gate[at] = v[:, :HID]
            dw_up[at] = v[:, HID:]

        @pl.when(i >= TILES)
        def _():
            dw_down[:, at] = dot(hid[...], xt[slot], ((0,), (0,))).astype(BF16)

    def at(ref, u, k, rows, kind, base=0):
        t, h = u // 2, lax.rem(u, 2)
        r = pl.multiple_of(base + t * ROWS + k * BLOCK, BLOCK)
        c = pl.multiple_of(h * WIDE + (WA if kind == "B" else 0), 128)
        return ref.at[pl.ds(r, rows * BLOCK), pl.ds(c, WB if kind == "B" else WA)]

    A = lambda ref, u, k, rows=1: at(ref, u, k, rows, "A")
    B = lambda ref, u, k, rows=1: at(ref, u, k, rows, "B")
    DA = lambda u, k: at(dx, u, k, 1, "A", core * HALF)
    DB = lambda u, k: at(dx, u, k, 1, "B", core * HALF)
    X = lambda u: lx.at[pl.ds(pl.multiple_of(u * BLOCK, BLOCK), BLOCK)]
    val = lambda ref: ref[...].astype(F32)
    mo, ms, no, ns = y * 2 + o, y * 2 + side, n * 2 + o, n * 2 + side
    se, sm, oe, om = side * 2, side * 2 + 1, o * 2, o * 2 + 1

    def same(ref, s, r, to):
        return remote(ref, ref, s, r, to)

    def got(ref, r):
        remote(ref, ref, sib_s.at[0, 0], r, sibling).wait_recv()

    end_sends = dict(
        lA=lambda u: same(A(lr, u, n * 2, 2), sA.at[u, 0], rrA.at[u], rung),
        lB=lambda u: same(B(lz, u, o * 2, 2), sB.at[u, 0], rzB.at[u, 0], inner),
        lX=lambda u: remote(B(lz, u, sm), X(u), sB.at[u, 1], rxB.at[u], inner),
        Amo=lambda u: same(A(lz, u, mo), sA.at[u, 1], rzA.at[u, 0], inner),
        Ams=lambda u: same(DA(u, ms), sA.at[u, 2], bA.at[u, ms], inner),
        AmsR=lambda u: same(DA(u, ms), sA.at[u, 3], bA.at[u, ms], rung),
        Bse=lambda u: remote(B(lz, u, se), B(lr, u, se), sB.at[u, 2], rrB.at[u], rung),
        Bse2=lambda u: same(DB(u, se), sB.at[u, 3], bB.at[u, se], inner),
        bAmo=lambda u: same(DA(u, mo), sA.at[u, 4], bA.at[u, mo], rung),
    )
    mid_sends = dict(
        lA=lambda u: same(A(lr, u, n * 2, 2), sA.at[u, 0], rrA.at[u], rung),
        Bo=lambda u: same(B(lz, u, o * 2, 2), sB.at[u, 0], rzB.at[u, 1], inner),
        Amo=lambda u: same(A(lz, u, mo), sA.at[u, 1], rzA.at[u, 1], inner),
        BsO=lambda u: same(B(lz, u, se), sB.at[u, 1], rzB.at[u, 1], outer),
        BsR=lambda u: remote(B(lz, u, sm), B(lr, u, sm), sB.at[u, 2], rrB.at[u], rung),
        Ams=lambda u: same(A(lz, u, ms), sA.at[u, 2], rzA.at[u, 1], outer),
        Bsm2O=lambda u: same(DB(u, sm), sB.at[u, 3], bB.at[u, sm], outer),
        Bsm2I=lambda u: same(DB(u, sm), sB.at[u, 4], bB.at[u, sm], inner),
        bAmsI=lambda u: same(DA(u, ms), sA.at[u, 3], bA.at[u, ms], inner),
        bAmsR=lambda u: same(DA(u, ms), sA.at[u, 4], bA.at[u, ms], rung),
        bAmoO=lambda u: same(DA(u, mo), sA.at[u, 5], bA.at[u, mo], outer),
        bAmoR=lambda u: same(DA(u, mo), sA.at[u, 6], bA.at[u, mo], rung),
        bBse=lambda u: same(DB(u, se), sB.at[u, 5], bB.at[u, se], inner),
        bBom=lambda u: same(DB(u, om), sB.at[u, 6], bB.at[u, om], outer),
        bBoe=lambda u: same(DB(u, oe), sB.at[u, 7], bB.at[u, oe], outer),
    )

    def fin_copy(u):
        where = dx.at[pl.ds(mine(u // 2), ROWS), pl.ds(pl.multiple_of(lax.rem(u, 2) * WIDE, WIDE), WIDE)]
        return remote(where, where, fin_s.at[u], fin_r.at[u], sibling)

    def fin_wait(u):
        got(dx.at[pl.ds(theirs(u // 2), ROWS), pl.ds(pl.multiple_of(lax.rem(u, 2) * WIDE, WIDE), WIDE)],
            fin_r.at[u])

    def put(ref, v):
        ref[...] = v.astype(BF16)

    def ev_loc(u):
        t, h = u // 2, lax.rem(u, 2)
        for k in range(2):
            q = 2 * h + k
            sib_wait(t, q).wait_recv()
            r = pl.ds(pl.multiple_of(t * ROWS, ROWS), ROWS)
            loc[r, cols(q)] += dx[pl.ds(theirs(t), ROWS), cols(q)].astype(F32)
        pl.semaphore_signal(free.at[u], inc=1, device_id={"tp": sibling}, device_id_type=MESH)

    def ev_lA(sends):
        def f(u):
            put(A(lr, u, n * 2, 2), A(loc, u, n * 2, 2)[...])
            sends["lA"](u).start()
        return f

    def fin(u):
        pl.semaphore_wait(free.at[u], 1)
        fin_copy(u).start()

    def e_lB(u):
        put(B(lz, u, o * 2, 2), B(loc, u, o * 2, 2)[...])
        end_sends["lB"](u).start()
        put(B(lz, u, sm), B(loc, u, sm)[...])
        end_sends["lX"](u).start()

    def e_Amo(u):
        got(A(lr, u, y * 2, 2), rrA.at[u])
        put(A(lz, u, mo), A(loc, u, mo)[...] + val(A(lr, u, mo)))
        end_sends["Amo"](u).start()

    def e_Ams(u):
        got(A(lz, u, ms), rzA.at[u, 1])
        put(DA(u, ms), A(loc, u, ms)[...] + val(A(lr, u, ms)) + val(A(lz, u, ms)))
        end_sends["Ams"](u).start()
        end_sends["AmsR"](u).start()

    def e_Bse(u):
        got(B(lz, u, se), rzB.at[u, 1])
        put(B(lz, u, se), B(loc, u, se)[...] + val(B(lz, u, se)))
        end_sends["Bse"](u).start()

    def e_Bse2(u):
        got(B(lr, u, se), rrB.at[u])
        put(DB(u, se), val(B(lz, u, se)) + val(B(lr, u, se)))
        end_sends["Bse2"](u).start()

    def e_bAmo(u):
        got(DA(u, mo), bA.at[u, mo])
        end_sends["bAmo"](u).start()

    def e_fin(u):
        for k in (ns, no):
            got(DA(u, k), bA.at[u, k])
        for k in (sm, om, oe):
            got(DB(u, k), bB.at[u, k])
        fin(u)

    def m_Bo(u):
        got(B(lz, u, o * 2, 2), rzB.at[u, 0])
        put(B(lz, u, o * 2, 2), B(loc, u, o * 2, 2)[...] + val(B(lz, u, o * 2, 2)))
        mid_sends["Bo"](u).start()

    def m_Amo(u):
        got(A(lr, u, y * 2, 2), rrA.at[u])
        got(A(lz, u, mo), rzA.at[u, 0])
        put(A(lz, u, mo), A(loc, u, mo)[...] + val(A(lr, u, mo)) + val(A(lz, u, mo)))
        mid_sends["Amo"](u).start()

    def m_Bs(u):
        got(B(lz, u, side * 2, 2), rzB.at[u, 1])
        put(B(lz, u, se), B(loc, u, se)[...] + val(B(lz, u, se)))
        mid_sends["BsO"](u).start()
        got(X(u), rxB.at[u])
        put(B(lz, u, sm), B(loc, u, sm)[...] + val(B(lz, u, sm)) + val(X(u)))
        mid_sends["BsR"](u).start()

    def m_Ams(u):
        got(A(lz, u, ms), rzA.at[u, 1])
        put(A(lz, u, ms), A(loc, u, ms)[...] + val(A(lr, u, ms)) + val(A(lz, u, ms)))
        mid_sends["Ams"](u).start()

    def m_Bsm2(u):
        got(B(lr, u, sm), rrB.at[u])
        put(DB(u, sm), val(B(lz, u, sm)) + val(B(lr, u, sm)))
        mid_sends["Bsm2O"](u).start()
        mid_sends["Bsm2I"](u).start()

    def m_back(where, sem, k, names):
        def f(u):
            got(where(u, k), sem.at[u, k])
            for name in names:
                mid_sends[name](u).start()
        return f

    def m_fin(u):
        for k in (ns, no):
            got(DA(u, k), bA.at[u, k])
        fin(u)

    end_events = dict(loc=ev_loc, lA=ev_lA(end_sends), lB=e_lB, Amo=e_Amo, Ams=e_Ams, Bse=e_Bse,
                      Bse2=e_Bse2, bAmo=e_bAmo, fin=e_fin)
    mid_events = dict(loc=ev_loc, lA=ev_lA(mid_sends), Bo=m_Bo, Amo=m_Amo, Bs=m_Bs, Ams=m_Ams, Bsm2=m_Bsm2,
                      bAms=m_back(DA, bA, ms, ("bAmsI", "bAmsR")), bAmo=m_back(DA, bA, mo, ("bAmoO", "bAmoR")),
                      bBse=m_back(DB, bB, se, ("bBse",)), bBom=m_back(DB, bB, om, ("bBom",)),
                      bBoe=m_back(DB, bB, oe, ("bBoe",)), fin=m_fin)

    def events(i, pos):
        for here, when, handlers in ((is_end, END, end_events), (is_mid, MID, mid_events)):
            @pl.when(here)
            def _():
                for name, off in sorted(when.items(), key=lambda kv: kv[1]):
                    if int(off) % 2 == pos:
                        u = i - int(off) // 2

                        @pl.when((u >= 0) & (u < UNITS))
                        def _():
                            handlers[name](u)

    def body(i, carry):
        t, h = i // 2, lax.rem(i, 2)

        @pl.when((i < UNITS) & (h == 0))
        def _():
            @pl.when(t + 1 < STAGES)
            def _():
                load(t + 1)

            hidden_part(t)

            @pl.when(t == 0)
            def _():
                weights[1].wait()
                weights[2].wait()

        for pos in range(2):
            @pl.when(i < UNITS)
            def _():
                term_part(t, 2 * h + pos)

            if pos == 1:
                @pl.when(i == UNITS - 1)
                def _():
                    load_x(0)

            @pl.when((i >= UNITS) & (i < UNITS + TILES))
            def _():
                grad_part(2 * (i - UNITS) + pos)

            events(i, pos)
        return carry

    weights[0].wait()
    lax.fori_loop(0, LOOPS, body, 0)

    def drain(u, carry):
        @pl.when(is_end)
        def _():
            for send in end_sends.values():
                send(u).wait_send()

        @pl.when(is_mid)
        def _():
            for send in mid_sends.values():
                send(u).wait_send()

        fin_copy(u).wait_send()
        fin_wait(u)
        return carry

    lax.fori_loop(0, UNITS, drain, 0)
    for t in (STAGES - 2, STAGES - 1):
        for q in range(Q):
            sib_copy(t, q).wait_send()


def flush_kernel(*refs):
    sem = refs[-1]
    n = (len(refs) - 1) // 2
    copies = []
    for k in range(n):
        rows = refs[k].shape[0] // PARTS
        for p in range(PARTS):
            at = pl.ds(p * rows, rows)
            copies.append(pltpu.make_async_copy(refs[k].at[at], refs[n + k].at[at], sem.at[k, p]))
    for c in copies:
        c.start()
    for c in copies:
        c.wait()


def solution(mesh):
    dma = pltpu.SemaphoreType.DMA
    shapes = ((TOKENS, D), (D, HID), (D, HID), (HID, D))

    def step(x, dy, gate, up, w_gate, w_up, w_down):
        hbm = pl.BlockSpec(memory_space=pltpu.HBM)
        vmem = pl.BlockSpec(memory_space=pltpu.VMEM)
        held = pl.pallas_call(
            tree_kernel,
            out_shape=tuple(pltpu.VMEM(s, BF16) for s in shapes),
            in_specs=[hbm] * 7,
            out_specs=(vmem,) * 4,
            scratch_shapes=[
                pltpu.VMEM((2, 2 * ROWS, D), BF16),
                pltpu.VMEM((2, 2 * ROWS, HID), BF16), pltpu.VMEM((2, 2 * ROWS, HID), BF16),
                pltpu.VMEM((2, TOKENS, TILE), BF16),
                pltpu.VMEM((HALF, D), F32), pltpu.VMEM((2, ROWS, D), BF16),
                pltpu.VMEM((TOKENS, 2 * HID), BF16), pltpu.VMEM((TOKENS, HID), BF16),
                pltpu.VMEM((HALF, D), BF16), pltpu.VMEM((HALF, D), BF16),
                pltpu.VMEM((UNITS * BLOCK, WB), BF16),
                dma((3,)), dma((2, 6)), dma((2,)), pltpu.SemaphoreType.REGULAR((UNITS,)),
                dma((STAGES, Q)), dma((STAGES, Q)), dma((UNITS,)), dma((UNITS,)),
                dma((UNITS, 7)), dma((UNITS, 8)), dma((UNITS,)), dma((UNITS, 2)), dma((UNITS, 4)),
                dma((UNITS, 2)), dma((UNITS,)), dma((UNITS,)), dma((UNITS, 4)),
            ],
            compiler_params=pltpu.CompilerParams(
                collective_id=0, has_side_effects=True, vmem_limit_bytes=42 * 2**20),
        )(x, dy, gate, up, w_gate, w_up, w_down)
        return pl.pallas_call(
            flush_kernel,
            out_shape=tuple(jax.ShapeDtypeStruct(s, BF16) for s in shapes),
            in_specs=[vmem] * 4,
            out_specs=(hbm,) * 4,
            scratch_shapes=[dma((4, PARTS))],
            compiler_params=pltpu.CompilerParams(vmem_limit_bytes=2 * 2**20),
        )(*held)

    tokens, columns, rows = P("dp", None), P(None, "tp"), P("tp", None)
    return jax.shard_map(
        step,
        mesh=mesh,
        in_specs=(tokens, tokens, P("dp", "tp"), P("dp", "tp"), columns, columns, rows),
        out_specs=(tokens, P("dp", "tp"), P("dp", "tp"), P(("dp", "tp"), None)),
        check_vma=False,
    )
```

time: 140 us -> 137 us (0.979)
  Pallas kernels: 140 us -> 136 us
    pallas_call x1, Pallas kernels: 132 us -> 128 us  [step(): pl.pallas_call(tree_kernel, out_shape=tuple((pltpu.VMEM(s, BF16) for s in...]
where the time goes in v3:
time: 137 us
  Pallas kernels  136 us (99%)
    pallas_call x1, Pallas kernels, step(): pl.pallas_call(tree_kernel, out_shape=tuple((pltpu.VMEM(s, BF16) for s in...  128 us
    pallas_call x1, Pallas kernels, step(): pl.pallas_call(flush_kernel, out_shape=tuple((jax.ShapeDtypeStruct(s, BF1...  7.59 us

profile of v3, /device:TPU:0, one launch (start us, length us, event | category | flops | bytes accessed | tf_op | source)
XLA Modules:
  0.0 136.6 jit_solution(14173585000265816020)
XLA Ops:
  0.6 128.4 %shard_map.102 = (bf16[2048,3072]{1,0:T(8,128)(2,1)S(1)}, bf16[3072,512]{1,0:T(8,128)(2,1)S(1)}, bf16[3072,512]{1,0:T(8,128)(2,1)S(1)}, bf16[512,3072]{1,0:T(8,128)(2,1)S(1)}) custom-call(bf16[2048,3072]{1,0:T(8,128)(2,1)} %x.1, bf16[2048,3072]{1,0:T(8,128)(2,1)} %dy.1, bf16[2048,512]{1,0:T(8,128)(2,1)} %gate.1, bf16[2048,512]{1,0:T(8,128)(2,1)} %up.1, ...), custom_call_target="tpu_custom_call" | custom-call | tf_op jit(solution)/shard_map/pallas_call | solution.py:441
  129.0 7.6 %shard_map.103 = (bf16[2048,3072]{1,0:T(8,128)(2,1)}, bf16[3072,512]{1,0:T(8,128)(2,1)}, bf16[3072,512]{1,0:T(8,128)(2,1)}, bf16[512,3072]{1,0:T(8,128)(2,1)}) custom-call(bf16[2048,3072]{1,0:T(8,128)(2,1)S(1)} %get-tuple-element.8.refs_0_, bf16[3072,512]{1,0:T(8,128)(2,1)S(1)} %get-tuple-element.9.refs_1_, bf16[3072,512]{1,0:T(8,128)(2,1)S(1)} %get-tuple-element.10.refs_2_, ...), custom_call_target="tpu_custom_call" | custom-call | tf_op jit(solution)/shard_map/pallas_call | solution.py:462

commit v4 on v3

--- a/solution.py
+++ b/solution.py
@@ -17,15 +17,15 @@
 COLS = D // Q
 UNITS = 2 * STAGES
 WIDE = D // 2
-WA = 896
+WA = 1024
 WB = WIDE - WA
 TILE = 256
 TILES = D // TILE
 PARTS = 4
 
-END = dict(loc=2.0, lA=4.64, lB=2.47, Amo=11.33, Bse=10.53, Ams=32.77, Bse2=36.9, bAmo=43.27, fin=50)
-MID = dict(loc=2.0, lA=7.27, Bo=2.1, Amo=11.74, Bs=4.3, Ams=13.66, Bsm2=6.12, bAms=33.59, bAmo=36.27,
-           bBse=39.43, bBom=9.75, bBoe=45.08, fin=49.7)
+END = dict(loc=2.0, lA=2.1, lB=2.14, Amo=5.08, Bse=12.06, Ams=27.23, Bse2=33.68, bAmo=40.55, fin=52)
+MID = dict(loc=2.0, lA=5.51, Bo=7.82, Amo=10.23, Bs=10.22, Ams=12.07, Bsm2=12.39, bAms=32.1, bAmo=35.22,
+           bBse=39.16, bBom=14.54, bBoe=43.96, fin=48.63)
 LOOPS = UNITS + max(int(o) // 2 for o in (*END.values(), *MID.values()))
 
 

time: 137 us -> 133 us (0.971)
  Pallas kernels: 136 us -> 132 us
    pallas_call x1, Pallas kernels: 128 us -> 125 us  [step(): pl.pallas_call(tree_kernel, out_shape=tuple((pltpu.VMEM(s, BF16) for s in...]
where the time goes in v4:
time: 133 us
  Pallas kernels  132 us (99%)
    pallas_call x1, Pallas kernels, step(): pl.pallas_call(tree_kernel, out_shape=tuple((pltpu.VMEM(s, BF16) for s in...  125 us
    pallas_call x1, Pallas kernels, step(): pl.pallas_call(flush_kernel, out_shape=tuple((jax.ShapeDtypeStruct(s, BF1...  7.59 us

profile of v4, /device:TPU:0, one launch (start us, length us, event | category | flops | bytes accessed | tf_op | source)
XLA Modules:
  0.0 132.7 jit_solution(737096620664761182)
XLA Ops:
  0.6 124.5 %shard_map.102 = (bf16[2048,3072]{1,0:T(8,128)(2,1)S(1)}, bf16[3072,512]{1,0:T(8,128)(2,1)S(1)}, bf16[3072,512]{1,0:T(8,128)(2,1)S(1)}, bf16[512,3072]{1,0:T(8,128)(2,1)S(1)}) custom-call(bf16[2048,3072]{1,0:T(8,128)(2,1)} %x.1, bf16[2048,3072]{1,0:T(8,128)(2,1)} %dy.1, bf16[2048,512]{1,0:T(8,128)(2,1)} %gate.1, bf16[2048,512]{1,0:T(8,128)(2,1)} %up.1, ...), custom_call_target="tpu_custom_call" | custom-call | tf_op jit(solution)/shard_map/pallas_call | solution.py:441
  125.2 7.6 %shard_map.103 = (bf16[2048,3072]{1,0:T(8,128)(2,1)}, bf16[3072,512]{1,0:T(8,128)(2,1)}, bf16[3072,512]{1,0:T(8,128)(2,1)}, bf16[512,3072]{1,0:T(8,128)(2,1)}) custom-call(bf16[2048,3072]{1,0:T(8,128)(2,1)S(1)} %get-tuple-element.8.refs_0_, bf16[3072,512]{1,0:T(8,128)(2,1)S(1)} %get-tuple-element.9.refs_1_, bf16[3072,512]{1,0:T(8,128)(2,1)S(1)} %get-tuple-element.10.refs_2_, ...), custom_call_target="tpu_custom_call" | custom-call | tf_op jit(solution)/shard_map/pallas_call | solution.py:462

commit v5 on v4

--- a/solution.py
+++ b/solution.py
@@ -23,9 +23,9 @@
 TILES = D // TILE
 PARTS = 4
 
-END = dict(loc=2.0, lA=2.1, lB=2.14, Amo=5.08, Bse=12.06, Ams=27.23, Bse2=33.68, bAmo=40.55, fin=52)
-MID = dict(loc=2.0, lA=5.51, Bo=7.82, Amo=10.23, Bs=10.22, Ams=12.07, Bsm2=12.39, bAms=32.1, bAmo=35.22,
-           bBse=39.16, bBom=14.54, bBoe=43.96, fin=48.63)
+END = dict(loc=2.0, lA=3.73, lB=2.1, Amo=7.77, Bse=31.21, Ams=26.7, Bse2=34.23, bAmo=45.84, fin=56)
+MID = dict(loc=2.0, lA=3.9, Bo=4.2, Amo=9.93, Bs=6.44, Ams=12.45, Bsm2=9.38, bAms=28.53,
+           bAmo=31.94, fin=50.25, bBse=38.19, bBom=11.13, bBoe=44.03)
 LOOPS = UNITS + max(int(o) // 2 for o in (*END.values(), *MID.values()))
 
 

time: 133 us -> 131 us (0.985)
  Pallas kernels: 132 us -> 130 us
    pallas_call x1, Pallas kernels: 125 us -> 122 us  [step(): pl.pallas_call(tree_kernel, out_shape=tuple((pltpu.VMEM(s, BF16) for s in...]
where the time goes in v5:
time: 131 us
  Pallas kernels  130 us (99%)
    pallas_call x1, Pallas kernels, step(): pl.pallas_call(tree_kernel, out_shape=tuple((pltpu.VMEM(s, BF16) for s in...  122 us
    pallas_call x1, Pallas kernels, step(): pl.pallas_call(flush_kernel, out_shape=tuple((jax.ShapeDtypeStruct(s, BF1...  7.59 us

profile of v5, /device:TPU:0, one launch (start us, length us, event | category | flops | bytes accessed | tf_op | source)
XLA Modules:
  0.0 130.7 jit_solution(17357472689013353159)
XLA Ops:
  0.6 122.5 %shard_map.102 = (bf16[2048,3072]{1,0:T(8,128)(2,1)S(1)}, bf16[3072,512]{1,0:T(8,128)(2,1)S(1)}, bf16[3072,512]{1,0:T(8,128)(2,1)S(1)}, bf16[512,3072]{1,0:T(8,128)(2,1)S(1)}) custom-call(bf16[2048,3072]{1,0:T(8,128)(2,1)} %x.1, bf16[2048,3072]{1,0:T(8,128)(2,1)} %dy.1, bf16[2048,512]{1,0:T(8,128)(2,1)} %gate.1, bf16[2048,512]{1,0:T(8,128)(2,1)} %up.1, ...), custom_call_target="tpu_custom_call" | custom-call | tf_op jit(solution)/shard_map/pallas_call | solution.py:441
  123.1 7.6 %shard_map.103 = (bf16[2048,3072]{1,0:T(8,128)(2,1)}, bf16[3072,512]{1,0:T(8,128)(2,1)}, bf16[3072,512]{1,0:T(8,128)(2,1)}, bf16[512,3072]{1,0:T(8,128)(2,1)}) custom-call(bf16[2048,3072]{1,0:T(8,128)(2,1)S(1)} %get-tuple-element.8.refs_0_, bf16[3072,512]{1,0:T(8,128)(2,1)S(1)} %get-tuple-element.9.refs_1_, bf16[3072,512]{1,0:T(8,128)(2,1)S(1)} %get-tuple-element.10.refs_2_, ...), custom_call_target="tpu_custom_call" | custom-call | tf_op jit(solution)/shard_map/pallas_call | solution.py:462

commit v6 on v5

--- a/solution.py
+++ b/solution.py
@@ -230,13 +230,16 @@
         bBoe=lambda u: same(DB(u, oe), sB.at[u, 7], bB.at[u, oe], outer),
     )
 
-    def fin_copy(u):
-        where = dx.at[pl.ds(mine(u // 2), ROWS), pl.ds(pl.multiple_of(lax.rem(u, 2) * WIDE, WIDE), WIDE)]
-        return remote(where, where, fin_s.at[u], fin_r.at[u], sibling)
-
-    def fin_wait(u):
-        got(dx.at[pl.ds(theirs(u // 2), ROWS), pl.ds(pl.multiple_of(lax.rem(u, 2) * WIDE, WIDE), WIDE)],
-            fin_r.at[u])
+    def fin_at(u, k, row):
+        c = pl.multiple_of(lax.rem(u, 2) * WIDE + k * WA, 128)
+        return dx.at[pl.ds(row(u // 2), ROWS), pl.ds(c, (WA, WB)[k])]
+
+    def fin_copy(u, k):
+        where = fin_at(u, k, mine)
+        return remote(where, where, fin_s.at[u, k], fin_r.at[u, k], sibling)
+
+    def fin_wait(u, k):
+        got(fin_at(u, k, theirs), fin_r.at[u, k])
 
     def put(ref, v):
         ref[...] = v.astype(BF16)
@@ -256,10 +259,6 @@
             sends["lA"](u).start()
         return f
 
-    def fin(u):
-        pl.semaphore_wait(free.at[u], 1)
-        fin_copy(u).start()
-
     def e_lB(u):
         put(B(lz, u, o * 2, 2), B(loc, u, o * 2, 2)[...])
         end_sends["lB"](u).start()
@@ -292,11 +291,13 @@
         end_sends["bAmo"](u).start()
 
     def e_fin(u):
+        pl.semaphore_wait(free.at[u], 1)
+        for k in (sm, om, oe):
+            got(DB(u, k), bB.at[u, k])
+        fin_copy(u, 1).start()
         for k in (ns, no):
             got(DA(u, k), bA.at[u, k])
-        for k in (sm, om, oe):
-            got(DB(u, k), bB.at[u, k])
-        fin(u)
+        fin_copy(u, 0).start()
 
     def m_Bo(u):
         got(B(lz, u, o * 2, 2), rzB.at[u, 0])
@@ -336,9 +337,11 @@
         return f
 
     def m_fin(u):
+        pl.semaphore_wait(free.at[u], 1)
+        fin_copy(u, 1).start()
         for k in (ns, no):
             got(DA(u, k), bA.at[u, k])
-        fin(u)
+        fin_copy(u, 0).start()
 
     end_events = dict(loc=ev_loc, lA=ev_lA(end_sends), lB=e_lB, Amo=e_Amo, Ams=e_Ams, Bse=e_Bse,
                       Bse2=e_Bse2, bAmo=e_bAmo, fin=e_fin)
@@ -406,8 +409,9 @@
             for send in mid_sends.values():
                 send(u).wait_send()
 
-        fin_copy(u).wait_send()
-        fin_wait(u)
+        for k in range(2):
+            fin_copy(u, k).wait_send()
+            fin_wait(u, k)
         return carry
 
     lax.fori_loop(0, UNITS, drain, 0)
@@ -452,7 +456,7 @@
                 pltpu.VMEM((HALF, D), BF16), pltpu.VMEM((HALF, D), BF16),
                 pltpu.VMEM((UNITS * BLOCK, WB), BF16),
                 dma((3,)), dma((2, 6)), dma((2,)), pltpu.SemaphoreType.REGULAR((UNITS,)),
-                dma((STAGES, Q)), dma((STAGES, Q)), dma((UNITS,)), dma((UNITS,)),
+                dma((STAGES, Q)), dma((STAGES, Q)), dma((UNITS, 2)), dma((UNITS, 2)),
                 dma((UNITS, 7)), dma((UNITS, 8)), dma((UNITS,)), dma((UNITS, 2)), dma((UNITS, 4)),
                 dma((UNITS, 2)), dma((UNITS,)), dma((UNITS,)), dma((UNITS, 4)),
             ],

time: 131 us -> 131 us (level)
  no operation moved by 1% of the time
where the time goes in v6:
time: 131 us
  Pallas kernels  130 us (99%)
    pallas_call x1, Pallas kernels, step(): pl.pallas_call(tree_kernel, out_shape=tuple((pltpu.VMEM(s, BF16) for s in...  123 us
    pallas_call x1, Pallas kernels, step(): pl.pallas_call(flush_kernel, out_shape=tuple((jax.ShapeDtypeStruct(s, BF1...  7.59 us

profile of v6, /device:TPU:0, one launch (start us, length us, event | category | flops | bytes accessed | tf_op | source)
XLA Modules:
  0.0 131.0 jit_solution(17134917790513207963)
XLA Ops:
  0.6 122.8 %shard_map.102 = (bf16[2048,3072]{1,0:T(8,128)(2,1)S(1)}, bf16[3072,512]{1,0:T(8,128)(2,1)S(1)}, bf16[3072,512]{1,0:T(8,128)(2,1)S(1)}, bf16[512,3072]{1,0:T(8,128)(2,1)S(1)}) custom-call(bf16[2048,3072]{1,0:T(8,128)(2,1)} %x.1, bf16[2048,3072]{1,0:T(8,128)(2,1)} %dy.1, bf16[2048,512]{1,0:T(8,128)(2,1)} %gate.1, bf16[2048,512]{1,0:T(8,128)(2,1)} %up.1, ...), custom_call_target="tpu_custom_call" | custom-call | tf_op jit(solution)/shard_map/pallas_call | solution.py:445
  123.4 7.6 %shard_map.103 = (bf16[2048,3072]{1,0:T(8,128)(2,1)}, bf16[3072,512]{1,0:T(8,128)(2,1)}, bf16[3072,512]{1,0:T(8,128)(2,1)}, bf16[512,3072]{1,0:T(8,128)(2,1)}) custom-call(bf16[2048,3072]{1,0:T(8,128)(2,1)S(1)} %get-tuple-element.8.refs_0_, bf16[3072,512]{1,0:T(8,128)(2,1)S(1)} %get-tuple-element.9.refs_1_, bf16[3072,512]{1,0:T(8,128)(2,1)S(1)} %get-tuple-element.10.refs_2_, ...), custom_call_target="tpu_custom_call" | custom-call | tf_op jit(solution)/shard_map/pallas_call | solution.py:466
